TPU v7x, 256 devices: a 4x2x16 block of a 4x16x16 slice. The times are simulated.
256 devices in a mesh: rep: 2 (over y), gx: 128 (over x, z, core).
Axes of the slice: x: 4, y: 2, z: 16, core: 2. Of those that a mesh axis runs over, the one named last changes fastest.
The devices are a block of a 4x16x16 slice.
Arguments:
- positions: float32 [3, 262144], P(None, ('rep', 'gx')), parts along dimension 1, may hold values from 0 to 8, as said below
- field: float32 [3, 262144], P(None, ('rep', 'gx')), parts along dimension 1, may hold values from -45 to 45
- inv_polar: float32 [262144], P(('rep', 'gx')), parts along dimension 0, may hold values from 2 to 8
- x_spline: float32 [2, 5, 262144], P(None, None, ('rep', 'gx')), parts along dimension 2, may hold values from -1 to 1, as said below
- yz_spline: float32 [4, 262144, 128], P(None, ('rep', 'gx')), parts along dimension 1, may hold values from -1 to 1, as said below
- tile_list: int32 [2048, 7], P(('rep', 'gx')), parts along dimension 0, may hold values from 0 to 13, as said below
- tile_count: int32 [2048], P(('rep', 'gx')), parts along dimension 0, may hold values from 1 to 7, as said below
Outputs:
- dipoles: float32 [3, 262144], P(None, ('rep', 'gx')), parts along dimension 1
- residual: float32 [3, 262144], P(None, ('rep', 'gx')), parts along dimension 1
There are 2 independent parts, one for each index of `rep`. A program takes and returns all parts, laid end to end along the dimension named above; each array names one. Nothing has to cross between parts.
Inputs may be any that keep to these rules, and one draw needn't show every extreme that they name: `positions`: the first coordinate of an atom of block b of its slab lies in [b, b + 1); the other two lie in [0, 2). x_spline[0, k, i] and x_spline[1, k, i] are the cardinal B-spline of order 5 and its derivative at u_i + 4 - k for some u_i in [0, 1). `yz_spline`: rows 0 and 1 hold, for each atom, the cardinal B-spline of order 5 and its derivative at u + 4 - k placed at grid line (t + k) mod 128 for k < 5, for some start t and some u in [0, 1), and zero elsewhere; rows 2 and 3 likewise with their own start and offset. `tile_list`: row g = s * 8 + b lists in rising order the extended blocks b + 3 + e, -3 <= e <= 3, for which global blocks g and g + e (modulo 1024) are neighbours; being neighbours is symmetric and always holds for e = 0; entries from tile_count[g] on equal b + 3. `tile_count`: global block 0 has all 7 neighbours.
All inputs are finite; a program needn't handle non-finite values.
Results may differ from a plain program's by a relative error of at most 0.0003.
Values sent between devices are 32-bit elements; how exact they have to be, the bound alone decides.
A program may use at most 64 MiB of HBM per device.

v0:
```python
import jax
import jax.numpy as jnp
from jax import lax
from jax.sharding import Mesh
from jax.sharding import PartitionSpec as P

GRID = 128
ORDER = 5
TILE = 128
HALO_BLK = 3
ITERS = 3
GX = ("gx_0", "gx_1", "gx_2")
REP_GX = ("rep", "gx_0", "gx_1", "gx_2")
PAIR_C = 0.025
RECIP_C = 8192.0
DAMP = 0.0008
EXACT = lax.Precision.HIGHEST


def from_behind(x, axis, by):
    devices = lax.axis_size(axis)
    return lax.ppermute(x, axis, [(i, (i + by) % devices) for i in range(devices)])


def extended(x, sides, width):
    for axis, dim in sides:
        devices, length = (lax.axis_size(axis), x.shape[dim])
        up = [(i, (i + 1) % devices) for i in range(devices)]
        down = [(j, i) for i, j in up]
        last = lax.slice_in_dim(x, length - width, length, axis=dim)
        first = lax.slice_in_dim(x, 0, width, axis=dim)
        before = lax.ppermute(last, axis, up)
        after = lax.ppermute(first, axis, down)
        x = jnp.concatenate([before, x, after], axis=dim)
    return x


def split_up(x, dim, devices):
    before, after = (x.shape[:dim], x.shape[dim + 1 :])
    return jnp.moveaxis(x.reshape(*before, devices, -1, *after), dim, 0)


def in_order(tiles, dim):
    dims = list(tiles.shape[1:])
    dims[dim] *= tiles.shape[0]
    return jnp.moveaxis(tiles, 0, dim).reshape(dims)


def turned_blocks(tiles, axes, sequence):
    dims = [lax.axis_size(a) for a in axes]
    tiles = tiles.reshape(*dims, *tiles.shape[1:])
    for k in sequence:
        tiles = lax.all_to_all(tiles, axes[k], split_axis=k, concat_axis=k, tiled=True)
    return tiles.reshape(-1, *tiles.shape[len(axes) :])


def exchange_by_chip(x, groups, sequence, split_dim, concat_dim):
    devices = lax.axis_size(groups[0]) * lax.axis_size(groups[1])
    tiles = split_up(x, split_dim, devices)
    return in_order(turned_blocks(tiles, groups, sequence), concat_dim)


def over_axes(x, axes):
    for axis in axes:
        x = lax.psum(x, axis)
    return x


def pair_field(home_pos, ext_pos, ext_vec, tile_rows, live_counts):
    slab_blocks = home_pos.shape[1] // TILE
    ext_blocks = ext_pos.shape[1] // TILE
    home_blocks = home_pos.reshape(3, slab_blocks, TILE).transpose(1, 0, 2)
    pos_blocks = ext_pos.reshape(3, ext_blocks, TILE)
    vec_blocks = ext_vec.reshape(3, ext_blocks, TILE)
    slot_index = jnp.arange(tile_rows.shape[1], dtype=jnp.int32)
    self_pair = jnp.eye(TILE, dtype=bool)

    def one_block(carried, scan_item):
        home_block, tile_row, live_count, block_index = scan_item
        near_pos = jnp.take(pos_blocks, tile_row, axis=1)
        near_vec = jnp.take(vec_blocks, tile_row, axis=1)
        offsets = home_block[:, None, :, None] - near_pos[:, :, None, :]
        distance_sq = jnp.sum(offsets * offsets, axis=0) + 1.0
        inverse = lax.rsqrt(distance_sq)
        third_power = inverse * inverse * inverse
        fifth_power = third_power * inverse * inverse
        same_block = (tile_row == block_index + HALO_BLK)[:, None, None]
        live_mask = (slot_index < live_count)[:, None, None] & ~(same_block & self_pair[None])
        third_power = jnp.where(live_mask, third_power, 0.0)
        fifth_power = jnp.where(live_mask, fifth_power, 0.0)
        projection = jnp.sum(offsets * near_vec[:, :, None, :], axis=0)
        field_sum = jnp.sum(
            third_power[None] * near_vec[:, :, None, :]
            - 3.0 * (fifth_power * projection)[None] * offsets,
            axis=(1, 3),
        )
        return (carried, PAIR_C * field_sum)

    block_ids = jnp.arange(slab_blocks, dtype=jnp.int32)
    unused_carry, blocks_out = lax.scan(
        one_block, jnp.zeros((), jnp.float32), (home_blocks, tile_rows, live_counts, block_ids)
    )
    return blocks_out.transpose(1, 0, 2).reshape(3, slab_blocks * TILE)


def slab_weights(local_plane, x_spline, planes):
    spline_steps = jnp.arange(ORDER, dtype=jnp.int32)
    plane_index = jnp.arange(planes, dtype=jnp.int32)
    matches = local_plane[None, :, None] + spline_steps[:, None, None] == plane_index[None, None, :]
    spline_value = jnp.sum(jnp.where(matches, x_spline[0][:, :, None], 0.0), axis=0)
    spline_slope = jnp.sum(jnp.where(matches, x_spline[1][:, :, None], 0.0), axis=0)
    return (spline_value, spline_slope)


def spread_dipoles(vector, spline_value, spline_slope, yz_spline):
    atoms_here = spline_value.shape[0]
    planes = spline_value.shape[1]
    grid_lines = yz_spline.shape[2]
    lead_terms = (vector[0][:, None] * spline_slope)[:, :, None] * yz_spline[0][:, None, :]
    lead_terms = (
        lead_terms + (vector[1][:, None] * spline_value)[:, :, None] * yz_spline[1][:, None, :]
    )
    tail_terms = (vector[2][:, None] * spline_value)[:, :, None] * yz_spline[0][:, None, :]
    contract = (((0,), (0,)), ((), ()))
    charge = lax.dot_general(
        lead_terms.reshape(atoms_here, planes * grid_lines), yz_spline[2], contract, precision=EXACT
    )
    charge = charge + lax.dot_general(
        tail_terms.reshape(atoms_here, planes * grid_lines), yz_spline[3], contract, precision=EXACT
    )
    return charge.reshape(planes, grid_lines, grid_lines)


def gather_field(potential, spline_value, spline_slope, yz_spline):
    planes = potential.shape[0]
    grid_lines = potential.shape[1]
    atoms_here = spline_value.shape[0]
    flat_grid = potential.reshape(planes * grid_lines, grid_lines)
    contract = (((1,), (1,)), ((), ()))
    plain_sum = lax.dot_general(yz_spline[2], flat_grid, contract, precision=EXACT).reshape(
        atoms_here, planes, grid_lines
    )
    tilted_sum = lax.dot_general(yz_spline[3], flat_grid, contract, precision=EXACT).reshape(
        atoms_here, planes, grid_lines
    )
    first_comp = jnp.sum(
        spline_slope[:, :, None] * yz_spline[0][:, None, :] * plain_sum, axis=(1, 2)
    )
    second_comp = jnp.sum(
        spline_value[:, :, None] * yz_spline[1][:, None, :] * plain_sum, axis=(1, 2)
    )
    third_comp = jnp.sum(
        spline_value[:, :, None] * yz_spline[0][:, None, :] * tilted_sum, axis=(1, 2)
    )
    return jnp.stack([first_comp, second_comp, third_comp])


def mode_of(freq, size):
    half_size = size // 2
    mode_num = jnp.where(freq <= half_size, freq, freq - half_size)
    weight = jnp.where((freq == 0) | (freq == half_size), 1.0 / size, 2.0 / size)
    return (mode_num.astype(jnp.float32), weight.astype(jnp.float32))


def basis_rows(size, points):
    freq = jnp.arange(size, dtype=jnp.int32)
    half_size = size // 2
    mode_num = jnp.where(freq <= half_size, freq, freq - half_size)
    phase = mode_num[:, None] * points[None, :] % size
    angle = phase.astype(jnp.float32) * (2.0 * jnp.pi / size)
    return jnp.where((freq <= half_size)[:, None], jnp.cos(angle), jnp.sin(angle))


def kernel_block(x_modes, x_weights, y_modes, y_weights, z_modes, z_weights):
    mode_sq = (
        x_modes[:, None, None] * x_modes[:, None, None]
        + y_modes[None, :, None] * y_modes[None, :, None]
        + z_modes[None, None, :] * z_modes[None, None, :]
    )
    safe_sq = jnp.where(mode_sq > 0, mode_sq, 1.0)
    green = jnp.where(mode_sq > 0, RECIP_C * jnp.exp(-DAMP * safe_sq) / safe_sq, 0.0)
    return green * x_weights[:, None, None] * y_weights[None, :, None] * z_weights[None, None, :]


def forward_lines(charge, fourier_rows):
    along_z = jnp.einsum("pyz,kz->pyk", charge, fourier_rows, precision=EXACT)
    return jnp.einsum("jy,pyk->pjk", fourier_rows, along_z, precision=EXACT)


def inverse_lines(spectrum, fourier_rows):
    along_z = jnp.einsum("pjk,kz->pjz", spectrum, fourier_rows, precision=EXACT)
    return jnp.einsum("jy,pjz->pyz", fourier_rows, along_z, precision=EXACT)


def from_above(piece, distance):
    return from_behind(piece, GX, -distance)


def from_below(piece, distance):
    return from_behind(piece, GX, distance)


def per_device(positions, field, inv_polar, x_spline, yz_spline, tile_list, tile_count):
    rank_count = lax.axis_size(GX)
    rank_index = lax.axis_index(GX)
    atoms_here = positions.shape[1]
    planes = GRID // rank_count
    extent = planes + 4
    halo_atoms = HALO_BLK * TILE
    slab_blocks = atoms_here // TILE
    local_plane = jnp.arange(atoms_here, dtype=jnp.int32) * planes // atoms_here
    spline_value, spline_slope = slab_weights(local_plane, x_spline, extent)
    ext_pos = extended(positions, ((GX, 1),), halo_atoms)
    shift_x = jnp.concatenate(
        [
            jnp.full((halo_atoms,), -1.0 * slab_blocks, jnp.float32),
            jnp.zeros((atoms_here,), jnp.float32),
            jnp.full((halo_atoms,), 1.0 * slab_blocks, jnp.float32),
        ]
    )
    ext_pos = ext_pos.at[0].add(shift_x)
    fourier_rows = basis_rows(GRID, jnp.arange(GRID, dtype=jnp.int32))
    ky_count = GRID // rank_count
    all_freq = jnp.arange(GRID, dtype=jnp.int32)
    ky_freq = rank_index * ky_count + jnp.arange(ky_count, dtype=jnp.int32)
    full_modes, full_weights = mode_of(all_freq, GRID)
    ky_modes, ky_weights = mode_of(ky_freq, GRID)
    kernel = kernel_block(full_modes, full_weights, ky_modes, ky_weights, full_modes, full_weights)
    kernel = kernel.reshape(GRID, ky_count * GRID)

    def reciprocal(charge):
        rim_planes = min(2, planes)
        hop_count = (planes + 1) // planes
        owned_planes = charge[2 : 2 + planes]
        for distance in range(1, hop_count + 1):
            lower_piece = charge[2 - distance * rim_planes : 2 - (distance - 1) * rim_planes]
            owned_planes = owned_planes.at[planes - rim_planes :].add(
                from_above(lower_piece, distance)
            )
            upper_piece = charge[
                planes + 2 + (distance - 1) * rim_planes : planes + 2 + distance * rim_planes
            ]
            owned_planes = owned_planes.at[:rim_planes].add(from_below(upper_piece, distance))
        spectrum = forward_lines(owned_planes, fourier_rows)
        pencils = exchange_by_chip(spectrum, (("gx_0", "gx_1"), "gx_2"), (1, 0), 1, 0)
        flat_pencils = pencils.reshape(GRID, ky_count * GRID)
        spectral_lines = jnp.dot(fourier_rows, flat_pencils, precision=EXACT) * kernel
        returned_lines = lax.dot_general(
            fourier_rows, spectral_lines, (((0,), (0,)), ((), ())), precision=EXACT
        )
        returned = exchange_by_chip(
            returned_lines.reshape(GRID, ky_count, GRID), (("gx_0", "gx_1"), "gx_2"), (1, 0), 0, 1
        )
        own_potential = inverse_lines(returned, fourier_rows)
        below_parts = [from_below(own_potential, distance) for distance in range(hop_count, 0, -1)]
        above_parts = [from_above(own_potential, distance) for distance in range(1, hop_count + 1)]
        return jnp.concatenate(below_parts + [own_potential] + above_parts, axis=0)

    def apply(vector):
        ext_vec = extended(vector, ((GX, 1),), halo_atoms)
        near_field = pair_field(positions, ext_pos, ext_vec, tile_list, tile_count)
        charge = spread_dipoles(vector, spline_value, spline_slope, yz_spline)
        far_field = gather_field(reciprocal(charge), spline_value, spline_slope, yz_spline)
        return inv_polar[None, :] * vector + far_field - near_field

    def paired(residual, precond, applied):
        return (
            over_axes(jnp.sum(residual * precond), GX),
            over_axes(jnp.sum(applied * precond), GX),
        )

    dipoles = jnp.zeros_like(field)
    residual = field
    precond = field / inv_polar[None, :]
    applied = apply(precond)
    rz_now, curvature = paired(residual, precond, applied)
    step_size = rz_now / curvature
    direction = precond
    applied_dir = applied
    for sweep_index in range(ITERS):
        dipoles = dipoles + step_size * direction
        residual = residual - step_size * applied_dir
        if sweep_index + 1 < ITERS:
            precond = residual / inv_polar[None, :]
            applied = apply(precond)
            rz_next, curvature = paired(residual, precond, applied)
            beta_ratio = rz_next / rz_now
            step_size = rz_next / (curvature - beta_ratio * rz_next / step_size)
            direction = precond + beta_ratio * direction
            applied_dir = applied + beta_ratio * applied_dir
            rz_now = rz_next
    return (dipoles, residual)


def solution(mesh):
    torus = Mesh(mesh.devices.reshape(mesh.shape["rep"], 4, 16, 2), ("rep", "gx_0", "gx_1", "gx_2"))
    in_specs = (
        P(None, REP_GX),
        P(None, REP_GX),
        P(REP_GX),
        P(None, None, REP_GX),
        P(None, REP_GX, None),
        P(REP_GX, None),
        P(REP_GX),
    )
    out_specs = (P(None, REP_GX), P(None, REP_GX))
    return jax.shard_map(
        per_device, mesh=torus, in_specs=in_specs, out_specs=out_specs, check_vma=False
    )
```

profile of v0, /device:TPU:33, one launch (start us, length us, event | category | flops | bytes accessed | tf_op | source)
XLA Modules:
  0.0 596.3 jit_solution(14503698682587773255)
XLA Ops:
  5.5 5.2 broadcast_multiply_fusion.3
  10.8 2.2 fusion.64
  13.0 2.2 convolution_add_fusion.2
  15.9 20.4 %collective-permute-start = (f32[1,128,128]{2,1,0:T(8,128)}, f32[1,128,128]{2,1,0:T(8,128)}, u32[]{:S(2)}, u32[]{:S(2)}) collective-permute-start(f32[1,128,128]{2,1,0:T(8,128)} %get-tuple-element.678), channel_id=1, source_target_pairs={{0,127},{1,0},{2,1},{3,2},{4,3},{5,4},{6,5},{7,6},{8,7},{9,8},{10,... | collective-permute-start | bytes 196616 | tf_op jit(solution)/shard_map/ppermute | solution.py:22
  36.4 10.2 %collective-permute-start.2 = (f32[1,128,128]{2,1,0:T(8,128)}, f32[1,128,128]{2,1,0:T(8,128)}, u32[]{:S(2)}, u32[]{:S(2)}) collective-permute-start(f32[1,128,128]{2,1,0:T(8,128)} %get-tuple-element.680), channel_id=1, source_target_pairs={{0,126},{1,127},{2,0},{3,1},{4,2},{5,3},{6,4},{7,5},{8,6},{9,7},{1... | collective-permute-start | bytes 196616 | tf_op jit(solution)/shard_map/ppermute | solution.py:22
  52.5 3.7 collective-permute-start.11
  56.2 1.5 fusion.102
  59.0 8.5 %all_to_all.60 = f32[64,2,1,1,128]{4,0,3,2,1:T(8,128)S(1)} all-to-all(f32[64,2,1,1,128]{4,0,3,2,1:T(8,128)S(1)} %copy.68), channel_id=1, replica_groups=mesh['rep'=2,'gx_0'=4,'gx_1'=16,'gx_2'=2] {'gx_2'}, dimensions={1} | all-to-all | bytes 131072 | tf_op jit(solution)/shard_map/all_to_all | solution.py:53
  68.2 6.5 %all-to-all-start.1 = ((f32[64,2,1,1,128]{4,1,3,2,0:T(2,128)}), f32[64,2,1,1,128]{4,1,3,2,0:T(2,128)S(1)}, u32[]{:S(2)}, u32[]{:S(2)}) async-start(f32[64,2,1,1,128]{4,1,3,2,0:T(2,128)} %copy.69), calls=%async_computation.1 | async-start | bytes 131072 | tf_op jit(solution)/shard_map/all_to_all | solution.py:53
  76.1 10.7 %all-to-all-done.1 = f32[64,2,1,1,128]{4,1,3,2,0:T(2,128)S(1)} async-done(((f32[64,2,1,1,128]{4,1,3,2,0:T(2,128)}), f32[64,2,1,1,128]{4,1,3,2,0:T(2,128)S(1)}, u32[]{:S(2)}, u32[]{:S(2)}) %all-to-all-start.1) | async-done | bytes 65568 | tf_op jit(solution)/shard_map/all_to_all | solution.py:53
  89.4 5.4 all_to_all.61
  95.5 6.5 %all-to-all-start.3 = ((f32[64,2,1,1,128]{4,1,3,2,0:T(2,128)}), f32[64,2,1,1,128]{4,1,3,2,0:T(2,128)S(1)}, u32[]{:S(2)}, u32[]{:S(2)}) async-start(f32[64,2,1,1,128]{4,1,3,2,0:T(2,128)} %copy.71), calls=%async_computation.3 | async-start | bytes 131072 | tf_op jit(solution)/shard_map/all_to_all | solution.py:53
  103.5 10.6 %all-to-all-done.3 = f32[64,2,1,1,128]{4,1,3,2,0:T(2,128)S(1)} async-done(((f32[64,2,1,1,128]{4,1,3,2,0:T(2,128)}), f32[64,2,1,1,128]{4,1,3,2,0:T(2,128)S(1)}, u32[]{:S(2)}, u32[]{:S(2)}) %all-to-all-start.3) | async-done | bytes 65568 | tf_op jit(solution)/shard_map/all_to_all | solution.py:53
  115.8 43.6 %while.58 = (s32[]{:T(128)}, f32[8,3,128]{2,1,0:T(4,128)S(1)}, s32[8]{0:T(128)S(1)}, s32[8,7]{1,0:T(8,128)}, s32[8]{0:T(128)S(1)}, /*index=5*/f32[8,3,128]{2,1,0...) while((s32[]{:T(128)}, f32[8,3,128]{2,1,0:T(4,128)S(1)}, ...), condition=%wide.region_13.15_spmd.clone, body=%wide.region_9.14_spmd.clone.sunk | while | flops 4610363 | bytes 3891027 | solution.py:100
  159.4 2.8 collective-permute-start.5
  162.2 4.5 collective-permute-start.7
  166.8 1.5 collective-permute-done.7
  168.3 3.3 fusion.45
  171.7 4.3 fusion.47
  176.7 6.7 %all-reduce.5 = (f32[]{:T(128)}, f32[]{:T(128)}) all-reduce(f32[]{:T(128)} %get-tuple-element.562, f32[]{:T(128)} %get-tuple-element.561), channel_id=1, replica_groups=mesh['rep'=2,'gx_0'=4,'gx_1'=16,'gx_2'=2] {'gx_0'}, use_global_device_ids=true, to_apply=%region_1.2 | all-reduce | flops 2 | bytes 16 | tf_op jit(solution)/shard_map/psum | solution.py:65
  183.3 26.5 %all-reduce.2 = (f32[]{:T(128)}, f32[]{:T(128)}) all-reduce(f32[]{:T(128)} %get-tuple-element.621, f32[]{:T(128)} %get-tuple-element.622), channel_id=1, replica_groups=mesh['rep'=2,'gx_0'=4,'gx_1'=16,'gx_2'=2] {'gx_1'}, use_global_device_ids=true, to_apply=%region_2.3 | all-reduce | flops 2 | bytes 16 | tf_op jit(solution)/shard_map/psum | solution.py:65
  209.9 13.9 %all-reduce.8 = (f32[]{:T(128)}, f32[]{:T(128)}) all-reduce(f32[]{:T(128)} %get-tuple-element.615, f32[]{:T(128)} %get-tuple-element.616), channel_id=1, replica_groups=mesh['rep'=2,'gx_0'=4,'gx_1'=16,'gx_2'=2] {'gx_2'}, use_global_device_ids=true, to_apply=%region_3.4 | all-reduce | flops 2 | bytes 16 | tf_op jit(solution)/shard_map/psum | solution.py:65
  225.3 1.9 broadcast_multiply_fusion.1
  227.2 2.2 fusion.60
  229.5 2.2 convolution_add_fusion.1
  232.2 1.8 collective-permute-start.13
  234.0 3.4 collective-permute-start.14
  238.7 5.1 collective-permute-done.15
  245.0 3.5 all_to_all.62
  248.5 17.8 %all_to_all.63 = f32[64,2,1,1,128]{4,1,3,2,0:T(2,128)S(1)} all-to-all(f32[64,2,1,1,128]{4,1,3,2,0:T(2,128)S(1)} %copy.75), channel_id=1, replica_groups=mesh['rep'=2,'gx_0'=4,'gx_1'=16,'gx_2'=2] {'gx_0','gx_1'}, dimensions={0} | all-to-all | bytes 131072 | tf_op jit(solution)/shard_map/all_to_all | solution.py:53
  267.5 5.5 all_to_all.64
  273.6 6.5 %all-to-all-start.7 = ((f32[64,2,1,1,128]{4,1,3,2,0:T(2,128)}), f32[64,2,1,1,128]{4,1,3,2,0:T(2,128)S(1)}, u32[]{:S(2)}, u32[]{:S(2)}) async-start(f32[64,2,1,1,128]{4,1,3,2,0:T(2,128)} %copy.77), calls=%async_computation.7 | async-start | bytes 131072 | tf_op jit(solution)/shard_map/all_to_all | solution.py:53
  281.7 2.6 collective-permute-done.21
  284.3 7.9 %all-to-all-done.7 = f32[64,2,1,1,128]{4,1,3,2,0:T(2,128)S(1)} async-done(((f32[64,2,1,1,128]{4,1,3,2,0:T(2,128)}), f32[64,2,1,1,128]{4,1,3,2,0:T(2,128)S(1)}, u32[]{:S(2)}, u32[]{:S(2)}) %all-to-all-start.7) | async-done | bytes 65568 | tf_op jit(solution)/shard_map/all_to_all | solution.py:53
  294.4 48.8 %while.59 = (s32[]{:T(128)}, f32[8,3,128]{2,1,0:T(4,128)S(1)}, s32[8]{0:T(128)S(1)}, s32[8,7]{1,0:T(8,128)}, s32[8]{0:T(128)}, /*index=5*/f32[8,3,128]{2,1,0:T(4...) while((s32[]{:T(128)}, f32[8,3,128]{2,1,0:T(4,128)S(1)}, ...), condition=%wide.region_29.31_spmd.clone, body=%wide.region_25.30_spmd.clone.sunk | while | flops 4610363 | bytes 3891339 | solution.py:100
  343.2 3.0 collective-permute-start.17
  346.2 4.3 collective-permute-start.19
  351.9 5.1 fusion.43
  357.0 3.3 fusion.42
  360.3 1.4 multiply_reduce_fusion.2
  361.7 6.8 %all-reduce.4 = (f32[]{:T(128)}, f32[]{:T(128)}) all-reduce(f32[]{:T(128)} %get-tuple-element.560, f32[]{:T(128)} %get-tuple-element.559), channel_id=1, replica_groups=mesh['rep'=2,'gx_0'=4,'gx_1'=16,'gx_2'=2] {'gx_0'}, use_global_device_ids=true, to_apply=%region_19.21 | all-reduce | flops 2 | bytes 16 | tf_op jit(solution)/shard_map/psum | solution.py:65
  368.4 26.8 %all-reduce.1 = (f32[]{:T(128)}, f32[]{:T(128)}) all-reduce(f32[]{:T(128)} %get-tuple-element.619, f32[]{:T(128)} %get-tuple-element.620), channel_id=1, replica_groups=mesh['rep'=2,'gx_0'=4,'gx_1'=16,'gx_2'=2] {'gx_1'}, use_global_device_ids=true, to_apply=%region_20.22 | all-reduce | flops 2 | bytes 16 | tf_op jit(solution)/shard_map/psum | solution.py:65
  395.2 14.1 %all-reduce.7 = (f32[]{:T(128)}, f32[]{:T(128)}) all-reduce(f32[]{:T(128)} %get-tuple-element.613, f32[]{:T(128)} %get-tuple-element.614), channel_id=1, replica_groups=mesh['rep'=2,'gx_0'=4,'gx_1'=16,'gx_2'=2] {'gx_2'}, use_global_device_ids=true, to_apply=%region_21.23 | all-reduce | flops 2 | bytes 16 | tf_op jit(solution)/shard_map/psum | solution.py:65
  414.1 1.9 broadcast_multiply_fusion
  416.1 2.2 fusion.56
  418.3 2.2 convolution_add_fusion
  421.0 1.4 collective-permute-start.23
  422.4 3.4 collective-permute-start.24
  427.2 5.1 collective-permute-done.25
  433.4 3.5 all_to_all.65
  437.0 18.2 %all_to_all.66 = f32[64,2,1,1,128]{4,1,3,2,0:T(2,128)S(1)} all-to-all(f32[64,2,1,1,128]{4,1,3,2,0:T(2,128)S(1)} %copy.81), channel_id=1, replica_groups=mesh['rep'=2,'gx_0'=4,'gx_1'=16,'gx_2'=2] {'gx_0','gx_1'}, dimensions={0} | all-to-all | bytes 131072 | tf_op jit(solution)/shard_map/all_to_all | solution.py:53
  456.4 5.3 all_to_all.67
  462.4 6.4 %all-to-all-start.11 = ((f32[64,2,1,1,128]{4,1,3,2,0:T(2,128)}), f32[64,2,1,1,128]{4,1,3,2,0:T(2,128)S(1)}, u32[]{:S(2)}, u32[]{:S(2)}) async-start(f32[64,2,1,1,128]{4,1,3,2,0:T(2,128)} %copy.83), calls=%async_computation.11 | async-start | bytes 131072 | tf_op jit(solution)/shard_map/all_to_all | solution.py:53
  470.5 2.6 collective-permute-done.31
  473.2 7.8 %all-to-all-done.11 = f32[64,2,1,1,128]{4,1,3,2,0:T(2,128)S(1)} async-done(((f32[64,2,1,1,128]{4,1,3,2,0:T(2,128)}), f32[64,2,1,1,128]{4,1,3,2,0:T(2,128)S(1)}, u32[]{:S(2)}, u32[]{:S(2)}) %all-to-all-start.11) | async-done | bytes 65568 | tf_op jit(solution)/shard_map/all_to_all | solution.py:53
  482.7 43.5 %while.60 = (s32[]{:T(128)}, f32[8,3,128]{2,1,0:T(4,128)S(1)}, s32[8]{0:T(128)S(1)}, s32[8,7]{1,0:T(8,128)}, s32[8]{0:T(128)S(1)}, /*index=5*/f32[8,3,128]{2,1,0...) while((s32[]{:T(128)}, f32[8,3,128]{2,1,0:T(4,128)S(1)}, ...), condition=%wide.region_45.47_spmd.clone, body=%wide.region_41.46_spmd.clone.sunk | while | flops 4610363 | bytes 3891027 | solution.py:100
  526.2 2.7 collective-permute-start.27
  529.0 4.7 collective-permute-start.29
  533.7 1.5 collective-permute-done.29
  535.3 5.1 fusion.40
  540.4 3.3 fusion.39
  544.4 6.7 %all-reduce.3 = (f32[]{:T(128)}, f32[]{:T(128)}) all-reduce(f32[]{:T(128)} %get-tuple-element.558, f32[]{:T(128)} %get-tuple-element.557), channel_id=1, replica_groups=mesh['rep'=2,'gx_0'=4,'gx_1'=16,'gx_2'=2] {'gx_0'}, use_global_device_ids=true, to_apply=%region_35.37 | all-reduce | flops 2 | bytes 16 | tf_op jit(solution)/shard_map/psum | solution.py:65
  551.1 26.5 %all-reduce = (f32[]{:T(128)}, f32[]{:T(128)}) all-reduce(f32[]{:T(128)} %get-tuple-element.617, f32[]{:T(128)} %get-tuple-element.618), channel_id=1, replica_groups=mesh['rep'=2,'gx_0'=4,'gx_1'=16,'gx_2'=2] {'gx_1'}, use_global_device_ids=true, to_apply=%region_36.38 | all-reduce | flops 2 | bytes 16 | tf_op jit(solution)/shard_map/psum | solution.py:65
  577.6 13.9 %all-reduce.6 = (f32[]{:T(128)}, f32[]{:T(128)}) all-reduce(f32[]{:T(128)} %get-tuple-element.611, f32[]{:T(128)} %get-tuple-element.612), channel_id=1, replica_groups=mesh['rep'=2,'gx_0'=4,'gx_1'=16,'gx_2'=2] {'gx_2'}, use_global_device_ids=true, to_apply=%region_37.39 | all-reduce | flops 2 | bytes 16 | tf_op jit(solution)/shard_map/psum | solution.py:65
  (581 shorter events, 160.2 us)
Async XLA Ops:
  5.5 5.3 copy-start.1
  13.0 33.6 %copy-start.5 = (f32[3,1024]{1,0:T(4,128)S(1)}, f32[3,1024]{1,0:T(4,128)}, u32[]{:S(2)}) copy-start(f32[3,1024]{1,0:T(4,128)} %param.65) | copy-start | bytes 36868
  15.9 34.8 %collective-permute-start = (f32[1,128,128]{2,1,0:T(8,128)}, f32[1,128,128]{2,1,0:T(8,128)}, u32[]{:S(2)}, u32[]{:S(2)}) collective-permute-start(f32[1,128,128]{2,1,0:T(8,128)} %get-tuple-element.678), channel_id=1, source_target_pairs={{0,127},{1,0},{2,1},{3,2},{4,3},{5,4},{6,5},{7,6},{8,7},{9,8},{10,... | collective-permute-start | bytes 196616 | tf_op jit(solution)/shard_map/ppermute | solution.py:22
  36.4 14.9 %collective-permute-start.1 = (f32[1,128,128]{2,1,0:T(8,128)}, f32[1,128,128]{2,1,0:T(8,128)}, u32[]{:S(2)}, u32[]{:S(2)}) collective-permute-start(f32[1,128,128]{2,1,0:T(8,128)} %get-tuple-element.681), channel_id=1, source_target_pairs={{0,1},{1,2},{2,3},{3,4},{4,5},{5,6},{6,7},{7,8},{8,9},{9,10},{10,1... | collective-permute-start | bytes 196616 | tf_op jit(solution)/shard_map/ppermute | solution.py:22
  36.4 16.1 %collective-permute-start.2 = (f32[1,128,128]{2,1,0:T(8,128)}, f32[1,128,128]{2,1,0:T(8,128)}, u32[]{:S(2)}, u32[]{:S(2)}) collective-permute-start(f32[1,128,128]{2,1,0:T(8,128)} %get-tuple-element.680), channel_id=1, source_target_pairs={{0,126},{1,127},{2,0},{3,1},{4,2},{5,3},{6,4},{7,5},{8,6},{9,7},{1... | collective-permute-start | bytes 196616 | tf_op jit(solution)/shard_map/ppermute | solution.py:22
  46.5 9.7 %collective-permute-start.3 = (f32[1,128,128]{2,1,0:T(8,128)}, f32[1,128,128]{2,1,0:T(8,128)}, u32[]{:S(2)}, u32[]{:S(2)}) collective-permute-start(f32[1,128,128]{2,1,0:T(8,128)} %get-tuple-element.679), channel_id=1, source_target_pairs={{0,2},{1,3},{2,4},{3,5},{4,6},{5,7},{6,8},{7,9},{8,10},{9,11},{10,... | collective-permute-start | bytes 196616 | tf_op jit(solution)/shard_map/ppermute | solution.py:22
  47.1 27.5 %collective-permute-start.8 = (f32[3,384]{1,0:T(4,128)}, f32[3,384]{1,0:T(4,128)}, u32[]{:S(2)}, u32[]{:S(2)}) collective-permute-start(f32[3,384]{1,0:T(4,128)} %get-tuple-element.708), channel_id=1, source_target_pairs={{0,1},{1,2},{2,3},{3,4},{4,5},{5,6},{6,7},{7,8},{8,9},{9,10},{10,1... | collective-permute-start | bytes 13832 | tf_op jit(solution)/shard_map/ppermute | solution.py:32
  50.7 24.7 %collective-permute-start.9 = (f32[3,384]{1,0:T(4,128)}, f32[3,384]{1,0:T(4,128)}, u32[]{:S(2)}, u32[]{:S(2)}) collective-permute-start(f32[3,384]{1,0:T(4,128)} %get-tuple-element.707), channel_id=1, source_target_pairs={{1,0},{2,1},{3,2},{4,3},{5,4},{6,5},{7,6},{8,7},{9,8},{10,9},{11,1... | collective-permute-start | bytes 13832 | tf_op jit(solution)/shard_map/ppermute | solution.py:33
  51.2 51.5 %collective-permute-start.10 = (f32[3,384]{1,0:T(4,128)}, f32[3,384]{1,0:T(4,128)}, u32[]{:S(2)}, u32[]{:S(2)}) collective-permute-start(f32[3,384]{1,0:T(4,128)} %get-tuple-element.705), channel_id=1, source_target_pairs={{0,1},{1,2},{2,3},{3,4},{4,5},{5,6},{6,7},{7,8},{8,9},{9,10},{10,1... | collective-permute-start | bytes 13832 | tf_op jit(solution)/shard_map/ppermute | solution.py:32
  52.5 50.3 %collective-permute-start.11 = (f32[3,384]{1,0:T(4,128)}, f32[3,384]{1,0:T(4,128)}, u32[]{:S(2)}, u32[]{:S(2)}) collective-permute-start(f32[3,384]{1,0:T(4,128)} %get-tuple-element.706), channel_id=1, source_target_pairs={{1,0},{2,1},{3,2},{4,3},{5,4},{6,5},{7,6},{8,7},{9,8},{10,9},{11,1... | collective-permute-start | bytes 13832 | tf_op jit(solution)/shard_map/ppermute | solution.py:33
  57.7 45.1 %copy-start.7 = (f32[3,1024]{1,0:T(4,128)S(1)}, f32[3,1024]{1,0:T(4,128)}, u32[]{:S(2)}) copy-start(f32[3,1024]{1,0:T(4,128)} %copy-done.6) | copy-start | bytes 36868
  57.7 56.4 %copy-start.22 = (s32[128]{0:T(128)S(1)}, s32[128]{0:T(128)}, u32[]{:S(2)}) copy-start(s32[128]{0:T(128)} %add_select_fusion.3) | copy-start | bytes 1540
  57.7 56.4 %copy-start.25 = (pred[128]{0:T(512)(128)(4,1)S(1)}, pred[128]{0:T(512)(128)(4,1)}, u32[]{:S(2)}) copy-start(pred[128]{0:T(512)(128)(4,1)} %iota_compare_fusion.7) | copy-start | bytes 388
  57.8 58.0 %copy-start.10 = (s32[8]{0:T(128)S(1)}, s32[8]{0:T(128)}, u32[]{:S(2)}) copy-start(s32[8]{0:T(128)} %param.71) | copy-start | bytes 100
  68.2 18.6 %all-to-all-start.1 = ((f32[64,2,1,1,128]{4,1,3,2,0:T(2,128)}), f32[64,2,1,1,128]{4,1,3,2,0:T(2,128)S(1)}, u32[]{:S(2)}, u32[]{:S(2)}) async-start(f32[64,2,1,1,128]{4,1,3,2,0:T(2,128)} %copy.69), calls=%async_computation.1 | async-start | bytes 131072 | tf_op jit(solution)/shard_map/all_to_all | solution.py:53
  95.5 18.6 %all-to-all-start.3 = ((f32[64,2,1,1,128]{4,1,3,2,0:T(2,128)}), f32[64,2,1,1,128]{4,1,3,2,0:T(2,128)S(1)}, u32[]{:S(2)}, u32[]{:S(2)}) async-start(f32[64,2,1,1,128]{4,1,3,2,0:T(2,128)} %copy.71), calls=%async_computation.3 | async-start | bytes 131072 | tf_op jit(solution)/shard_map/all_to_all | solution.py:53
  115.3 51.5 %collective-permute-start.4 = (f32[1,128,128]{2,1,0:T(8,128)S(1)}, f32[1,128,128]{2,1,0:T(8,128)S(1)}, u32[]{:S(2)}, u32[]{:S(2)}) collective-permute-start(f32[1,128,128]{2,1,0:T(8,128)S(1)} %convolution_bitcast_fusion.2), channel_id=1, source_target_pairs={{0,2},{1,3},{2,4},{3,5},{4,6},{5,7},{6,8},{7,9},{8,10},{9,11},{10,... | collective-permute-start | bytes 196616 | tf_op jit(solution)/shard_map/ppermute | solution.py:22
  159.4 12.2 %copy-start = (f32[1024,5,128]{0,2,1:T(8,128)S(1)}, f32[1024,5,128]{0,2,1:T(8,128)}, u32[]{:S(2)}) copy-start(f32[1024,5,128]{0,2,1:T(8,128)} %get-tuple-element.665) | copy-start | bytes 7864324
  159.4 7.3 %collective-permute-start.5 = (f32[1,128,128]{2,1,0:T(8,128)S(1)}, f32[1,128,128]{2,1,0:T(8,128)S(1)}, u32[]{:S(2)}, u32[]{:S(2)}) collective-permute-start(f32[1,128,128]{2,1,0:T(8,128)S(1)} %convolution_bitcast_fusion.2), channel_id=1, source_target_pairs={{0,1},{1,2},{2,3},{3,4},{4,5},{5,6},{6,7},{7,8},{8,9},{9,10},{10,1... | collective-permute-start | bytes 196616 | tf_op jit(solution)/shard_map/ppermute | solution.py:22
  162.2 4.6 collective-permute-start.6
  162.2 6.1 %collective-permute-start.7 = (f32[1,128,128]{2,1,0:T(8,128)S(1)}, f32[1,128,128]{2,1,0:T(8,128)S(1)}, u32[]{:S(2)}, u32[]{:S(2)}) collective-permute-start(f32[1,128,128]{2,1,0:T(8,128)S(1)} %convolution_bitcast_fusion.2), channel_id=1, source_target_pairs={{0,126},{1,127},{2,0},{3,1},{4,2},{5,3},{6,4},{7,5},{8,6},{9,7},{1... | collective-permute-start | bytes 196616 | tf_op jit(solution)/shard_map/ppermute | solution.py:22
  171.6 4.4 copy-start.4
  171.7 4.4 copy-start.8
  229.4 14.4 %copy-start.23 = (s32[128]{0:T(128)S(1)}, s32[128]{0:T(128)}, u32[]{:S(2)}) copy-start(s32[128]{0:T(128)} %add_select_fusion.3) | copy-start | bytes 1540
  229.4 14.4 %copy-start.26 = (pred[128]{0:T(512)(128)(4,1)S(1)}, pred[128]{0:T(512)(128)(4,1)}, u32[]{:S(2)}) copy-start(pred[128]{0:T(512)(128)(4,1)} %iota_compare_fusion.7) | copy-start | bytes 388
  229.4 36.9 %copy-start.16 = (f32[128]{0:T(128)S(1)}, f32[128]{0:T(128)}, u32[]{:S(2)}) copy-start(f32[128]{0:T(128)} %get-tuple-element.711) | copy-start | bytes 1540
  229.4 36.9 %copy-start.18 = (f32[128]{0:T(128)S(1)}, f32[128]{0:T(128)}, u32[]{:S(2)}) copy-start(f32[128]{0:T(128)} %get-tuple-element.712) | copy-start | bytes 1540
  229.4 36.9 %copy-start.20 = (f32[128]{0:T(128)S(1)}, f32[128]{0:T(128)}, u32[]{:S(2)}) copy-start(f32[128]{0:T(128)} %broadcast_add_fusion) | copy-start | bytes 1540
  231.7 62.8 %copy-start.11 = (s32[8]{0:T(128)S(1)}, s32[8]{0:T(128)}, u32[]{:S(2)}) copy-start(s32[8]{0:T(128)} %param.71) | copy-start | bytes 100
  231.7 5.7 collective-permute-start.12
  232.2 5.2 collective-permute-start.13
  234.0 4.7 collective-permute-start.14
  237.4 6.4 %collective-permute-start.15 = (f32[1,128,128]{2,1,0:T(8,128)S(1)}, f32[1,128,128]{2,1,0:T(8,128)S(1)}, u32[]{:S(2)}, u32[]{:S(2)}) collective-permute-start(f32[1,128,128]{2,1,0:T(8,128)S(1)} %get-tuple-element.675), channel_id=1, source_target_pairs={{0,2},{1,3},{2,4},{3,5},{4,6},{5,7},{6,8},{7,9},{8,10},{9,11},{10,... | collective-permute-start | bytes 196616 | tf_op jit(solution)/shard_map/ppermute | solution.py:22
  273.6 18.6 %all-to-all-start.7 = ((f32[64,2,1,1,128]{4,1,3,2,0:T(2,128)}), f32[64,2,1,1,128]{4,1,3,2,0:T(2,128)S(1)}, u32[]{:S(2)}, u32[]{:S(2)}) async-start(f32[64,2,1,1,128]{4,1,3,2,0:T(2,128)} %copy.77), calls=%async_computation.7 | async-start | bytes 131072 | tf_op jit(solution)/shard_map/all_to_all | solution.py:53
  280.1 1.6 collective-permute-start.20
  280.9 3.4 collective-permute-start.21
  293.4 57.1 %collective-permute-start.16 = (f32[1,128,128]{2,1,0:T(8,128)S(1)}, f32[1,128,128]{2,1,0:T(8,128)S(1)}, u32[]{:S(2)}, u32[]{:S(2)}) collective-permute-start(f32[1,128,128]{2,1,0:T(8,128)S(1)} %convolution_bitcast_fusion.1), channel_id=1, source_target_pairs={{0,2},{1,3},{2,4},{3,5},{4,6},{5,7},{6,8},{7,9},{8,10},{9,11},{10,... | collective-permute-start | bytes 196616 | tf_op jit(solution)/shard_map/ppermute | solution.py:22
  300.5 3.8 copy-start.12
  306.6 3.8 copy-start.12
  312.7 3.8 copy-start.12
  318.8 3.8 copy-start.12
  324.9 3.8 copy-start.12
  343.2 8.7 %copy-start.14 = (s32[8]{0:T(128)}, s32[8]{0:T(128)S(1)}, u32[]{:S(2)}) copy-start(s32[8]{0:T(128)S(1)} %get-tuple-element.1072) | copy-start | bytes 100
  343.2 13.8 %copy-start.9 = (f32[8,3,128]{2,1,0:T(4,128)}, f32[8,3,128]{2,1,0:T(4,128)S(1)}, u32[]{:S(2)}) copy-start(f32[8,3,128]{2,1,0:T(4,128)S(1)} %get-tuple-element.412) | copy-start | bytes 36868
  343.2 7.3 %collective-permute-start.17 = (f32[1,128,128]{2,1,0:T(8,128)S(1)}, f32[1,128,128]{2,1,0:T(8,128)S(1)}, u32[]{:S(2)}, u32[]{:S(2)}) collective-permute-start(f32[1,128,128]{2,1,0:T(8,128)S(1)} %convolution_bitcast_fusion.1), channel_id=1, source_target_pairs={{0,1},{1,2},{2,3},{3,4},{4,5},{5,6},{6,7},{7,8},{8,9},{9,10},{10,1... | collective-permute-start | bytes 196616 | tf_op jit(solution)/shard_map/ppermute | solution.py:22
  346.2 4.4 collective-permute-start.18
  346.2 5.6 collective-permute-start.19
  418.3 14.0 %copy-start.24 = (s32[128]{0:T(128)S(1)}, s32[128]{0:T(128)}, u32[]{:S(2)}) copy-start(s32[128]{0:T(128)} %add_select_fusion.3) | copy-start | bytes 1540
  418.3 14.0 %copy-start.27 = (pred[128]{0:T(512)(128)(4,1)S(1)}, pred[128]{0:T(512)(128)(4,1)}, u32[]{:S(2)}) copy-start(pred[128]{0:T(512)(128)(4,1)} %iota_compare_fusion.7) | copy-start | bytes 388
  418.3 36.9 %copy-start.17 = (f32[128]{0:T(128)S(1)}, f32[128]{0:T(128)}, u32[]{:S(2)}) copy-start(f32[128]{0:T(128)} %get-tuple-element.711) | copy-start | bytes 1540
  418.3 36.9 %copy-start.19 = (f32[128]{0:T(128)S(1)}, f32[128]{0:T(128)}, u32[]{:S(2)}) copy-start(f32[128]{0:T(128)} %get-tuple-element.712) | copy-start | bytes 1540
  418.3 36.9 %copy-start.21 = (f32[128]{0:T(128)S(1)}, f32[128]{0:T(128)}, u32[]{:S(2)}) copy-start(f32[128]{0:T(128)} %broadcast_add_fusion) | copy-start | bytes 1540
  420.5 62.1 %copy-start.15 = (s32[8]{0:T(128)S(1)}, s32[8]{0:T(128)}, u32[]{:S(2)}) copy-start(s32[8]{0:T(128)} %copy-done.14) | copy-start | bytes 100
  420.6 5.3 collective-permute-start.22
  421.0 4.8 collective-permute-start.23
  422.4 4.7 collective-permute-start.24
  425.8 6.4 %collective-permute-start.25 = (f32[1,128,128]{2,1,0:T(8,128)S(1)}, f32[1,128,128]{2,1,0:T(8,128)S(1)}, u32[]{:S(2)}, u32[]{:S(2)}) collective-permute-start(f32[1,128,128]{2,1,0:T(8,128)S(1)} %get-tuple-element.671), channel_id=1, source_target_pairs={{0,2},{1,3},{2,4},{3,5},{4,6},{5,7},{6,8},{7,9},{8,10},{9,11},{10,... | collective-permute-start | bytes 196616 | tf_op jit(solution)/shard_map/ppermute | solution.py:22
  462.4 18.6 %all-to-all-start.11 = ((f32[64,2,1,1,128]{4,1,3,2,0:T(2,128)}), f32[64,2,1,1,128]{4,1,3,2,0:T(2,128)S(1)}, u32[]{:S(2)}, u32[]{:S(2)}) async-start(f32[64,2,1,1,128]{4,1,3,2,0:T(2,128)} %copy.83), calls=%async_computation.11 | async-start | bytes 131072 | tf_op jit(solution)/shard_map/all_to_all | solution.py:53
  468.8 1.7 collective-permute-start.30
  469.7 3.4 collective-permute-start.31
  482.1 51.5 %collective-permute-start.26 = (f32[1,128,128]{2,1,0:T(8,128)S(1)}, f32[1,128,128]{2,1,0:T(8,128)S(1)}, u32[]{:S(2)}, u32[]{:S(2)}) collective-permute-start(f32[1,128,128]{2,1,0:T(8,128)S(1)} %convolution_bitcast_fusion), channel_id=1, source_target_pairs={{0,2},{1,3},{2,4},{3,5},{4,6},{5,7},{6,8},{7,9},{8,10},{9,11},{10,... | collective-permute-start | bytes 196616 | tf_op jit(solution)/shard_map/ppermute | solution.py:22
  526.2 7.4 %collective-permute-start.27 = (f32[1,128,128]{2,1,0:T(8,128)S(1)}, f32[1,128,128]{2,1,0:T(8,128)S(1)}, u32[]{:S(2)}, u32[]{:S(2)}) collective-permute-start(f32[1,128,128]{2,1,0:T(8,128)S(1)} %convolution_bitcast_fusion), channel_id=1, source_target_pairs={{0,1},{1,2},{2,3},{3,4},{4,5},{5,6},{6,7},{7,8},{8,9},{9,10},{10,1... | collective-permute-start | bytes 196616 | tf_op jit(solution)/shard_map/ppermute | solution.py:22
  529.0 4.7 collective-permute-start.28
  529.0 6.3 %collective-permute-start.29 = (f32[1,128,128]{2,1,0:T(8,128)S(1)}, f32[1,128,128]{2,1,0:T(8,128)S(1)}, u32[]{:S(2)}, u32[]{:S(2)}) collective-permute-start(f32[1,128,128]{2,1,0:T(8,128)S(1)} %convolution_bitcast_fusion), channel_id=1, source_target_pairs={{0,126},{1,127},{2,0},{3,1},{4,2},{5,3},{6,4},{7,5},{8,6},{9,7},{1... | collective-permute-start | bytes 196616 | tf_op jit(solution)/shard_map/ppermute | solution.py:22
  (14 other events, 24.9 us)
where the time goes:
time: 608 us; the launch traced here: 596 us
  blocking collectives  210 us (35%)
  starting transfers between devices  98.1 us (16%)
  other arithmetic  74.3 us (12%)
  local copies, waits for them, and re-layouts  73.3 us (12%)
  waiting for transfers between devices  61.1 us (10%)
  matrix products  50.9 us (8%)
  loops' own time  17.2 us (3%)
  between operations  11.9 us (2%)
    psum x9, blocking collectives, over_axes(): x = lax.psum(x, axis)  142 us
    all_to_all x8, blocking collectives, turned_blocks(): lax.all_to_all(tiles, axes[k], split_axis=k, concat_axis=k, tiled=True)  67.7 us
    ppermute x24, starting transfers between devices, from_behind(): lax.ppermute(x, axis, [(i, (i + by) % devices) for i in range(devices)])  65.1 us
    all_to_all x4, waiting for transfers between devices, turned_blocks(): lax.all_to_all(tiles, axes[k], split_axis=k, concat_axis=k, tiled=True)  37.1 us
    dynamic_slice x48, local copies, waits for them, and re-layouts, pair_field(): lax.scan(one_block, jnp.zeros((), jnp.float32), (home_blocks, tile_rows,...  33.4 us
    and x24, other arithmetic, one_block(): near_pos = jnp.take(pos_blocks, tile_row, axis=1)  31.9 us
    all_to_all x4, starting transfers between devices, turned_blocks(): lax.all_to_all(tiles, axes[k], split_axis=k, concat_axis=k, tiled=True)  25.8 us
    another operation x3, loops' own time, pair_field(): lax.scan(one_block, jnp.zeros((), jnp.float32), (home_blocks, tile_rows,...  17.2 us
  transfers between devices with their start and end apart: 36, of which 15 were waited for; matrix products, arithmetic and copies ran while one was open for 22% of the time, Pallas kernels for 0%

commit v1 on v0

--- a/solution.py
+++ b/solution.py
@@ -62,7 +62,8 @@
 
 def over_axes(x, axes):
     for axis in axes:
-        x = lax.psum(x, axis)
+        pieces = lax.all_gather(x, axis)
+        x = jnp.sum(pieces, axis=0)
     return x
 
 

time: 608 us -> 641 us (1.054)
  local copies, waits for them, and re-layouts: 73.3 us -> 102 us
  other arithmetic: 74.3 us -> 85.1 us
    psum x9 -> x0, blocking collectives: 142 us -> none  [over_axes(): x = lax.psum(x, axis)]
    unnamed x0 -> x9, blocking collectives: none -> 136 us
    unnamed x66 -> x107, local copies, waits for them, and re-layouts: 1.51 us -> 29.6 us
    reduce_sum x0 -> x18, other arithmetic: none -> 10.9 us  [over_axes(): x = jnp.sum(pieces, axis=0)]
where the time goes in v1:
time: 641 us; the launch traced here: 629 us
  blocking collectives  204 us (32%)
  local copies, waits for them, and re-layouts  102 us (16%)
  starting transfers between devices  98 us (15%)
  other arithmetic  85.1 us (13%)
  waiting for transfers between devices  61 us (10%)
  matrix products  50.7 us (8%)
  loops' own time  16.7 us (3%)
  between operations  11.8 us (2%)
    unnamed x9, blocking collectives  136 us
    all_to_all x8, blocking collectives, turned_blocks(): lax.all_to_all(tiles, axes[k], split_axis=k, concat_axis=k, tiled=True)  67.7 us
    ppermute x24, starting transfers between devices, from_behind(): lax.ppermute(x, axis, [(i, (i + by) % devices) for i in range(devices)])  65 us
    all_to_all x4, waiting for transfers between devices, turned_blocks(): lax.all_to_all(tiles, axes[k], split_axis=k, concat_axis=k, tiled=True)  37.1 us
    dynamic_slice x48, local copies, waits for them, and re-layouts, pair_field(): lax.scan(one_block, jnp.zeros((), jnp.float32), (home_blocks, tile_rows,...  34.2 us
    and x24, other arithmetic, one_block(): near_pos = jnp.take(pos_blocks, tile_row, axis=1)  32 us
    unnamed x107, local copies, waits for them, and re-layouts  29.6 us
    all_to_all x4, starting transfers between devices, turned_blocks(): lax.all_to_all(tiles, axes[k], split_axis=k, concat_axis=k, tiled=True)  25.9 us
  transfers between devices with their start and end apart: 36, of which 15 were waited for; matrix products, arithmetic and copies ran while one was open for 22% of the time, Pallas kernels for 0%

profile of v1, /device:TPU:33, one launch (start us, length us, event | category | flops | bytes accessed | tf_op | source)
XLA Modules:
  0.0 629.1 jit_solution(666603174821779447)
XLA Ops:
  5.5 5.3 broadcast_multiply_fusion.3
  10.8 2.2 fusion.64
  13.0 2.2 convolution_add_fusion.2
  15.9 20.4 %collective-permute-start = (f32[1,128,128]{2,1,0:T(8,128)}, f32[1,128,128]{2,1,0:T(8,128)}, u32[]{:S(2)}, u32[]{:S(2)}) collective-permute-start(f32[1,128,128]{2,1,0:T(8,128)} %get-tuple-element.678), channel_id=1, source_target_pairs={{0,127},{1,0},{2,1},{3,2},{4,3},{5,4},{6,5},{7,6},{8,7},{9,8},{10,... | collective-permute-start | bytes 196616 | tf_op jit(solution)/shard_map/ppermute | solution.py:22
  36.4 10.2 %collective-permute-start.2 = (f32[1,128,128]{2,1,0:T(8,128)}, f32[1,128,128]{2,1,0:T(8,128)}, u32[]{:S(2)}, u32[]{:S(2)}) collective-permute-start(f32[1,128,128]{2,1,0:T(8,128)} %get-tuple-element.680), channel_id=1, source_target_pairs={{0,126},{1,127},{2,0},{3,1},{4,2},{5,3},{6,4},{7,5},{8,6},{9,7},{1... | collective-permute-start | bytes 196616 | tf_op jit(solution)/shard_map/ppermute | solution.py:22
  55.1 3.6 collective-permute-start.11
  58.7 1.5 fusion.102
  61.5 8.4 %all_to_all.60 = f32[64,2,1,1,128]{4,0,3,2,1:T(8,128)S(1)} all-to-all(f32[64,2,1,1,128]{4,0,3,2,1:T(8,128)S(1)} %copy.68), channel_id=1, replica_groups=mesh['rep'=2,'gx_0'=4,'gx_1'=16,'gx_2'=2] {'gx_2'}, dimensions={1} | all-to-all | bytes 131072 | tf_op jit(solution)/shard_map/all_to_all | solution.py:53
  70.5 6.5 %all-to-all-start.1 = ((f32[64,2,1,1,128]{4,1,3,2,0:T(2,128)}), f32[64,2,1,1,128]{4,1,3,2,0:T(2,128)S(1)}, u32[]{:S(2)}, u32[]{:S(2)}) async-start(f32[64,2,1,1,128]{4,1,3,2,0:T(2,128)} %copy.69), calls=%async_computation.1 | async-start | bytes 131072 | tf_op jit(solution)/shard_map/all_to_all | solution.py:53
  78.4 10.7 %all-to-all-done.1 = f32[64,2,1,1,128]{4,1,3,2,0:T(2,128)S(1)} async-done(((f32[64,2,1,1,128]{4,1,3,2,0:T(2,128)}), f32[64,2,1,1,128]{4,1,3,2,0:T(2,128)S(1)}, u32[]{:S(2)}, u32[]{:S(2)}) %all-to-all-start.1) | async-done | bytes 65568 | tf_op jit(solution)/shard_map/all_to_all | solution.py:53
  91.6 5.4 all_to_all.61
  97.7 6.5 %all-to-all-start.3 = ((f32[64,2,1,1,128]{4,1,3,2,0:T(2,128)}), f32[64,2,1,1,128]{4,1,3,2,0:T(2,128)S(1)}, u32[]{:S(2)}, u32[]{:S(2)}) async-start(f32[64,2,1,1,128]{4,1,3,2,0:T(2,128)} %copy.71), calls=%async_computation.3 | async-start | bytes 131072 | tf_op jit(solution)/shard_map/all_to_all | solution.py:53
  105.8 10.6 %all-to-all-done.3 = f32[64,2,1,1,128]{4,1,3,2,0:T(2,128)S(1)} async-done(((f32[64,2,1,1,128]{4,1,3,2,0:T(2,128)}), f32[64,2,1,1,128]{4,1,3,2,0:T(2,128)S(1)}, u32[]{:S(2)}, u32[]{:S(2)}) %all-to-all-start.3) | async-done | bytes 65568 | tf_op jit(solution)/shard_map/all_to_all | solution.py:53
  118.0 43.6 %while.58 = (s32[]{:T(128)}, f32[8,3,128]{2,1,0:T(4,128)S(1)}, s32[8]{0:T(128)S(1)}, s32[8,7]{1,0:T(8,128)}, s32[8]{0:T(128)S(1)}, /*index=5*/f32[8,3,128]{2,1,0...) while((s32[]{:T(128)}, f32[8,3,128]{2,1,0:T(4,128)S(1)}, ...), condition=%wide.region_13.15_spmd.clone, body=%wide.region_9.14_spmd.clone.sunk | while | flops 4610363 | bytes 3891027 | solution.py:101
  161.7 2.8 collective-permute-start.5
  164.5 4.5 collective-permute-start.7
  169.1 1.5 collective-permute-done.7
  170.6 3.3 fusion.45
  173.9 4.3 fusion.47
  178.9 1.4 dynamic-update-slice.27
  180.4 1.4 dynamic-update-slice.30
  182.5 6.0 all-reduce.23
  192.3 25.9 %all-reduce.20 = (f32[16]{0:T(128)S(1)}, f32[16]{0:T(128)S(1)}) all-reduce(f32[16]{0:T(128)S(1)} %dynamic-update-slice.28, f32[16]{0:T(128)S(1)} %dynamic-update-slice.31), channel_id=1, replica_groups=mesh['rep'=2,'gx_0'=4,'gx_1'=16,'gx_2'=2] {'gx_1'}, use_global_device_ids=true, to_apply=%add.1 | all-reduce | flops 32 | bytes 256
  222.2 13.2 %all-reduce.26 = (f32[2]{0:T(128)S(1)}, f32[2]{0:T(128)S(1)}) all-reduce(f32[2]{0:T(128)S(1)} %dynamic-update-slice.29, f32[2]{0:T(128)S(1)} %dynamic-update-slice.32), channel_id=1, replica_groups=mesh['rep'=2,'gx_0'=4,'gx_1'=16,'gx_2'=2] {'gx_2'}, use_global_device_ids=true, to_apply=%add.2 | all-reduce | flops 4 | bytes 32
  238.1 1.9 broadcast_multiply_fusion.1
  240.0 2.2 fusion.60
  242.2 2.2 convolution_add_fusion.1
  246.8 3.4 collective-permute-start.14
  251.5 5.1 collective-permute-done.15
  257.8 3.5 all_to_all.62
  261.3 17.8 %all_to_all.63 = f32[64,2,1,1,128]{4,1,3,2,0:T(2,128)S(1)} all-to-all(f32[64,2,1,1,128]{4,1,3,2,0:T(2,128)S(1)} %copy.75), channel_id=1, replica_groups=mesh['rep'=2,'gx_0'=4,'gx_1'=16,'gx_2'=2] {'gx_0','gx_1'}, dimensions={0} | all-to-all | bytes 131072 | tf_op jit(solution)/shard_map/all_to_all | solution.py:53
  280.3 5.5 all_to_all.64
  286.4 6.5 %all-to-all-start.7 = ((f32[64,2,1,1,128]{4,1,3,2,0:T(2,128)}), f32[64,2,1,1,128]{4,1,3,2,0:T(2,128)S(1)}, u32[]{:S(2)}, u32[]{:S(2)}) async-start(f32[64,2,1,1,128]{4,1,3,2,0:T(2,128)} %copy.77), calls=%async_computation.7 | async-start | bytes 131072 | tf_op jit(solution)/shard_map/all_to_all | solution.py:53
  294.5 2.6 collective-permute-done.21
  297.1 7.9 %all-to-all-done.7 = f32[64,2,1,1,128]{4,1,3,2,0:T(2,128)S(1)} async-done(((f32[64,2,1,1,128]{4,1,3,2,0:T(2,128)}), f32[64,2,1,1,128]{4,1,3,2,0:T(2,128)S(1)}, u32[]{:S(2)}, u32[]{:S(2)}) %all-to-all-start.7) | async-done | bytes 65568 | tf_op jit(solution)/shard_map/all_to_all | solution.py:53
  307.5 48.9 %while.59 = (s32[]{:T(128)}, f32[8,3,128]{2,1,0:T(4,128)S(1)}, s32[8]{0:T(128)S(1)}, s32[8,7]{1,0:T(8,128)}, s32[8]{0:T(128)}, /*index=5*/f32[8,3,128]{2,1,0:T(4...) while((s32[]{:T(128)}, f32[8,3,128]{2,1,0:T(4,128)S(1)}, ...), condition=%wide.region_29.31_spmd.clone, body=%wide.region_25.30_spmd.clone.sunk | while | flops 4610363 | bytes 3891339 | solution.py:101
  356.4 2.8 collective-permute-start.17
  359.2 4.3 collective-permute-start.19
  364.9 5.1 fusion.43
  370.0 3.3 fusion.42
  377.5 6.1 all-reduce.22
  387.4 26.1 %all-reduce.19 = (f32[16]{0:T(128)S(1)}, f32[16]{0:T(128)S(1)}) all-reduce(f32[16]{0:T(128)S(1)} %dynamic-update-slice.34, f32[16]{0:T(128)S(1)} %dynamic-update-slice.37), channel_id=1, replica_groups=mesh['rep'=2,'gx_0'=4,'gx_1'=16,'gx_2'=2] {'gx_1'}, use_global_device_ids=true, to_apply=%add.7 | all-reduce | flops 32 | bytes 256
  417.5 13.4 %all-reduce.25 = (f32[2]{0:T(128)S(1)}, f32[2]{0:T(128)S(1)}) all-reduce(f32[2]{0:T(128)S(1)} %dynamic-update-slice.35, f32[2]{0:T(128)S(1)} %dynamic-update-slice.38), channel_id=1, replica_groups=mesh['rep'=2,'gx_0'=4,'gx_1'=16,'gx_2'=2] {'gx_2'}, use_global_device_ids=true, to_apply=%add.8 | all-reduce | flops 4 | bytes 32
  436.8 1.9 broadcast_multiply_fusion
  438.7 2.2 fusion.56
  441.0 2.2 convolution_add_fusion
  445.1 3.4 collective-permute-start.24
  449.9 5.1 collective-permute-done.25
  456.1 3.5 all_to_all.65
  459.6 18.4 %all_to_all.66 = f32[64,2,1,1,128]{4,1,3,2,0:T(2,128)S(1)} all-to-all(f32[64,2,1,1,128]{4,1,3,2,0:T(2,128)S(1)} %copy.81), channel_id=1, replica_groups=mesh['rep'=2,'gx_0'=4,'gx_1'=16,'gx_2'=2] {'gx_0','gx_1'}, dimensions={0} | all-to-all | bytes 131072 | tf_op jit(solution)/shard_map/all_to_all | solution.py:53
  479.2 5.3 all_to_all.67
  485.2 6.5 %all-to-all-start.11 = ((f32[64,2,1,1,128]{4,1,3,2,0:T(2,128)}), f32[64,2,1,1,128]{4,1,3,2,0:T(2,128)S(1)}, u32[]{:S(2)}, u32[]{:S(2)}) async-start(f32[64,2,1,1,128]{4,1,3,2,0:T(2,128)} %copy.83), calls=%async_computation.11 | async-start | bytes 131072 | tf_op jit(solution)/shard_map/all_to_all | solution.py:53
  493.3 2.6 collective-permute-done.31
  496.0 7.8 %all-to-all-done.11 = f32[64,2,1,1,128]{4,1,3,2,0:T(2,128)S(1)} async-done(((f32[64,2,1,1,128]{4,1,3,2,0:T(2,128)}), f32[64,2,1,1,128]{4,1,3,2,0:T(2,128)S(1)}, u32[]{:S(2)}, u32[]{:S(2)}) %all-to-all-start.11) | async-done | bytes 65568 | tf_op jit(solution)/shard_map/all_to_all | solution.py:53
  505.5 43.7 %while.60 = (s32[]{:T(128)}, f32[8,3,128]{2,1,0:T(4,128)S(1)}, s32[8]{0:T(128)S(1)}, s32[8,7]{1,0:T(8,128)}, s32[8]{0:T(128)S(1)}, /*index=5*/f32[8,3,128]{2,1,0...) while((s32[]{:T(128)}, f32[8,3,128]{2,1,0:T(4,128)S(1)}, ...), condition=%wide.region_45.47_spmd.clone, body=%wide.region_41.46_spmd.clone.sunk | while | flops 4610363 | bytes 3891027 | solution.py:101
  549.3 2.8 collective-permute-start.27
  552.0 4.5 collective-permute-start.29
  558.1 5.1 fusion.40
  563.2 3.3 fusion.39
  567.2 1.4 dynamic-update-slice.42
  568.6 1.4 dynamic-update-slice.39
  570.0 6.0 all-reduce.21
  579.9 26.0 %all-reduce.18 = (f32[16]{0:T(128)S(1)}, f32[16]{0:T(128)S(1)}) all-reduce(f32[16]{0:T(128)S(1)} %dynamic-update-slice.40, f32[16]{0:T(128)S(1)} %dynamic-update-slice.43), channel_id=1, replica_groups=mesh['rep'=2,'gx_0'=4,'gx_1'=16,'gx_2'=2] {'gx_1'}, use_global_device_ids=true, to_apply=%add.13 | all-reduce | flops 32 | bytes 256
  609.9 13.2 %all-reduce.24 = (f32[2]{0:T(128)S(1)}, f32[2]{0:T(128)S(1)}) all-reduce(f32[2]{0:T(128)S(1)} %dynamic-update-slice.41, f32[2]{0:T(128)S(1)} %dynamic-update-slice.44), channel_id=1, replica_groups=mesh['rep'=2,'gx_0'=4,'gx_1'=16,'gx_2'=2] {'gx_2'}, use_global_device_ids=true, to_apply=%add.14 | all-reduce | flops 4 | bytes 32
  (640 shorter events, 200.2 us)
Async XLA Ops:
  5.5 5.3 copy-start.1
  13.0 33.6 %copy-start.5 = (f32[3,1024]{1,0:T(4,128)S(1)}, f32[3,1024]{1,0:T(4,128)}, u32[]{:S(2)}) copy-start(f32[3,1024]{1,0:T(4,128)} %param.65) | copy-start | bytes 36868
  15.9 37.2 %collective-permute-start = (f32[1,128,128]{2,1,0:T(8,128)}, f32[1,128,128]{2,1,0:T(8,128)}, u32[]{:S(2)}, u32[]{:S(2)}) collective-permute-start(f32[1,128,128]{2,1,0:T(8,128)} %get-tuple-element.678), channel_id=1, source_target_pairs={{0,127},{1,0},{2,1},{3,2},{4,3},{5,4},{6,5},{7,6},{8,7},{9,8},{10,... | collective-permute-start | bytes 196616 | tf_op jit(solution)/shard_map/ppermute | solution.py:22
  36.4 17.3 %collective-permute-start.1 = (f32[1,128,128]{2,1,0:T(8,128)}, f32[1,128,128]{2,1,0:T(8,128)}, u32[]{:S(2)}, u32[]{:S(2)}) collective-permute-start(f32[1,128,128]{2,1,0:T(8,128)} %get-tuple-element.681), channel_id=1, source_target_pairs={{0,1},{1,2},{2,3},{3,4},{4,5},{5,6},{6,7},{7,8},{8,9},{9,10},{10,1... | collective-permute-start | bytes 196616 | tf_op jit(solution)/shard_map/ppermute | solution.py:22
  36.4 18.8 %collective-permute-start.2 = (f32[1,128,128]{2,1,0:T(8,128)}, f32[1,128,128]{2,1,0:T(8,128)}, u32[]{:S(2)}, u32[]{:S(2)}) collective-permute-start(f32[1,128,128]{2,1,0:T(8,128)} %get-tuple-element.680), channel_id=1, source_target_pairs={{0,126},{1,127},{2,0},{3,1},{4,2},{5,3},{6,4},{7,5},{8,6},{9,7},{1... | collective-permute-start | bytes 196616 | tf_op jit(solution)/shard_map/ppermute | solution.py:22
  46.5 12.2 %collective-permute-start.3 = (f32[1,128,128]{2,1,0:T(8,128)}, f32[1,128,128]{2,1,0:T(8,128)}, u32[]{:S(2)}, u32[]{:S(2)}) collective-permute-start(f32[1,128,128]{2,1,0:T(8,128)} %get-tuple-element.679), channel_id=1, source_target_pairs={{0,2},{1,3},{2,4},{3,5},{4,6},{5,7},{6,8},{7,9},{8,10},{9,11},{10,... | collective-permute-start | bytes 196616 | tf_op jit(solution)/shard_map/ppermute | solution.py:22
  47.1 29.9 %collective-permute-start.8 = (f32[3,384]{1,0:T(4,128)}, f32[3,384]{1,0:T(4,128)}, u32[]{:S(2)}, u32[]{:S(2)}) collective-permute-start(f32[3,384]{1,0:T(4,128)} %get-tuple-element.708), channel_id=1, source_target_pairs={{0,1},{1,2},{2,3},{3,4},{4,5},{5,6},{6,7},{7,8},{8,9},{9,10},{10,1... | collective-permute-start | bytes 13832 | tf_op jit(solution)/shard_map/ppermute | solution.py:32
  53.2 24.5 %collective-permute-start.9 = (f32[3,384]{1,0:T(4,128)}, f32[3,384]{1,0:T(4,128)}, u32[]{:S(2)}, u32[]{:S(2)}) collective-permute-start(f32[3,384]{1,0:T(4,128)} %get-tuple-element.707), channel_id=1, source_target_pairs={{1,0},{2,1},{3,2},{4,3},{5,4},{6,5},{7,6},{8,7},{9,8},{10,9},{11,1... | collective-permute-start | bytes 13832 | tf_op jit(solution)/shard_map/ppermute | solution.py:33
  53.7 51.3 %collective-permute-start.10 = (f32[3,384]{1,0:T(4,128)}, f32[3,384]{1,0:T(4,128)}, u32[]{:S(2)}, u32[]{:S(2)}) collective-permute-start(f32[3,384]{1,0:T(4,128)} %get-tuple-element.705), channel_id=1, source_target_pairs={{0,1},{1,2},{2,3},{3,4},{4,5},{5,6},{6,7},{7,8},{8,9},{9,10},{10,1... | collective-permute-start | bytes 13832 | tf_op jit(solution)/shard_map/ppermute | solution.py:32
  55.1 49.9 %collective-permute-start.11 = (f32[3,384]{1,0:T(4,128)}, f32[3,384]{1,0:T(4,128)}, u32[]{:S(2)}, u32[]{:S(2)}) collective-permute-start(f32[3,384]{1,0:T(4,128)} %get-tuple-element.706), channel_id=1, source_target_pairs={{1,0},{2,1},{3,2},{4,3},{5,4},{6,5},{7,6},{8,7},{9,8},{10,9},{11,1... | collective-permute-start | bytes 13832 | tf_op jit(solution)/shard_map/ppermute | solution.py:33
  60.2 44.8 %copy-start.7 = (f32[3,1024]{1,0:T(4,128)S(1)}, f32[3,1024]{1,0:T(4,128)}, u32[]{:S(2)}) copy-start(f32[3,1024]{1,0:T(4,128)} %copy-done.6) | copy-start | bytes 36868
  60.2 56.1 %copy-start.23 = (s32[128]{0:T(128)S(1)}, s32[128]{0:T(128)}, u32[]{:S(2)}) copy-start(s32[128]{0:T(128)} %add_select_fusion.3) | copy-start | bytes 1540
  60.2 56.1 %copy-start.26 = (pred[128]{0:T(512)(128)(4,1)S(1)}, pred[128]{0:T(512)(128)(4,1)}, u32[]{:S(2)}) copy-start(pred[128]{0:T(512)(128)(4,1)} %iota_compare_fusion.7) | copy-start | bytes 388
  60.2 57.8 %copy-start.10 = (s32[8]{0:T(128)S(1)}, s32[8]{0:T(128)}, u32[]{:S(2)}) copy-start(s32[8]{0:T(128)} %param.71) | copy-start | bytes 100
  70.5 18.6 %all-to-all-start.1 = ((f32[64,2,1,1,128]{4,1,3,2,0:T(2,128)}), f32[64,2,1,1,128]{4,1,3,2,0:T(2,128)S(1)}, u32[]{:S(2)}, u32[]{:S(2)}) async-start(f32[64,2,1,1,128]{4,1,3,2,0:T(2,128)} %copy.69), calls=%async_computation.1 | async-start | bytes 131072 | tf_op jit(solution)/shard_map/all_to_all | solution.py:53
  97.7 18.6 %all-to-all-start.3 = ((f32[64,2,1,1,128]{4,1,3,2,0:T(2,128)}), f32[64,2,1,1,128]{4,1,3,2,0:T(2,128)S(1)}, u32[]{:S(2)}, u32[]{:S(2)}) async-start(f32[64,2,1,1,128]{4,1,3,2,0:T(2,128)} %copy.71), calls=%async_computation.3 | async-start | bytes 131072 | tf_op jit(solution)/shard_map/all_to_all | solution.py:53
  117.5 51.5 %collective-permute-start.4 = (f32[1,128,128]{2,1,0:T(8,128)S(1)}, f32[1,128,128]{2,1,0:T(8,128)S(1)}, u32[]{:S(2)}, u32[]{:S(2)}) collective-permute-start(f32[1,128,128]{2,1,0:T(8,128)S(1)} %convolution_bitcast_fusion.2), channel_id=1, source_target_pairs={{0,2},{1,3},{2,4},{3,5},{4,6},{5,7},{6,8},{7,9},{8,10},{9,11},{10,... | collective-permute-start | bytes 196616 | tf_op jit(solution)/shard_map/ppermute | solution.py:22
  161.7 12.2 %copy-start = (f32[1024,5,128]{0,2,1:T(8,128)S(1)}, f32[1024,5,128]{0,2,1:T(8,128)}, u32[]{:S(2)}) copy-start(f32[1024,5,128]{0,2,1:T(8,128)} %get-tuple-element.665) | copy-start | bytes 7864324
  161.7 7.3 %collective-permute-start.5 = (f32[1,128,128]{2,1,0:T(8,128)S(1)}, f32[1,128,128]{2,1,0:T(8,128)S(1)}, u32[]{:S(2)}, u32[]{:S(2)}) collective-permute-start(f32[1,128,128]{2,1,0:T(8,128)S(1)} %convolution_bitcast_fusion.2), channel_id=1, source_target_pairs={{0,1},{1,2},{2,3},{3,4},{4,5},{5,6},{6,7},{7,8},{8,9},{9,10},{10,1... | collective-permute-start | bytes 196616 | tf_op jit(solution)/shard_map/ppermute | solution.py:22
  164.5 4.6 collective-permute-start.6
  164.5 6.1 collective-permute-start.7
  173.9 4.4 copy-start.4
  173.9 4.4 copy-start.8
  173.9 7.9 %copy-start.16 = (u32[256]{0:T(256)S(1)}, u32[256]{0:T(256)}, u32[]{:S(2)}) copy-start(u32[256]{0:T(256)} %constant.571) | copy-start | bytes 3076
  242.2 14.4 %copy-start.24 = (s32[128]{0:T(128)S(1)}, s32[128]{0:T(128)}, u32[]{:S(2)}) copy-start(s32[128]{0:T(128)} %add_select_fusion.3) | copy-start | bytes 1540
  242.2 14.4 %copy-start.27 = (pred[128]{0:T(512)(128)(4,1)S(1)}, pred[128]{0:T(512)(128)(4,1)}, u32[]{:S(2)}) copy-start(pred[128]{0:T(512)(128)(4,1)} %iota_compare_fusion.7) | copy-start | bytes 388
  242.2 36.9 %copy-start.17 = (f32[128]{0:T(128)S(1)}, f32[128]{0:T(128)}, u32[]{:S(2)}) copy-start(f32[128]{0:T(128)} %get-tuple-element.711) | copy-start | bytes 1540
  242.2 36.9 %copy-start.19 = (f32[128]{0:T(128)S(1)}, f32[128]{0:T(128)}, u32[]{:S(2)}) copy-start(f32[128]{0:T(128)} %get-tuple-element.712) | copy-start | bytes 1540
  242.2 36.9 %copy-start.21 = (f32[128]{0:T(128)S(1)}, f32[128]{0:T(128)}, u32[]{:S(2)}) copy-start(f32[128]{0:T(128)} %broadcast_add_fusion) | copy-start | bytes 1540
  244.5 63.0 %copy-start.11 = (s32[8]{0:T(128)S(1)}, s32[8]{0:T(128)}, u32[]{:S(2)}) copy-start(s32[8]{0:T(128)} %param.71) | copy-start | bytes 100
  244.5 5.7 collective-permute-start.12
  245.4 4.8 collective-permute-start.13
  246.8 4.7 collective-permute-start.14
  250.2 6.4 %collective-permute-start.15 = (f32[1,128,128]{2,1,0:T(8,128)S(1)}, f32[1,128,128]{2,1,0:T(8,128)S(1)}, u32[]{:S(2)}, u32[]{:S(2)}) collective-permute-start(f32[1,128,128]{2,1,0:T(8,128)S(1)} %get-tuple-element.675), channel_id=1, source_target_pairs={{0,2},{1,3},{2,4},{3,5},{4,6},{5,7},{6,8},{7,9},{8,10},{9,11},{10,... | collective-permute-start | bytes 196616 | tf_op jit(solution)/shard_map/ppermute | solution.py:22
  286.4 18.6 %all-to-all-start.7 = ((f32[64,2,1,1,128]{4,1,3,2,0:T(2,128)}), f32[64,2,1,1,128]{4,1,3,2,0:T(2,128)S(1)}, u32[]{:S(2)}, u32[]{:S(2)}) async-start(f32[64,2,1,1,128]{4,1,3,2,0:T(2,128)} %copy.77), calls=%async_computation.7 | async-start | bytes 131072 | tf_op jit(solution)/shard_map/all_to_all | solution.py:53
  292.9 1.6 collective-permute-start.20
  293.7 3.4 collective-permute-start.21
  306.2 57.3 %collective-permute-start.16 = (f32[1,128,128]{2,1,0:T(8,128)S(1)}, f32[1,128,128]{2,1,0:T(8,128)S(1)}, u32[]{:S(2)}, u32[]{:S(2)}) collective-permute-start(f32[1,128,128]{2,1,0:T(8,128)S(1)} %convolution_bitcast_fusion.1), channel_id=1, source_target_pairs={{0,2},{1,3},{2,4},{3,5},{4,6},{5,7},{6,8},{7,9},{8,10},{9,11},{10,... | collective-permute-start | bytes 196616 | tf_op jit(solution)/shard_map/ppermute | solution.py:22
  313.6 3.8 copy-start.12
  319.7 3.8 copy-start.12
  325.8 3.8 copy-start.12
  338.0 3.8 copy-start.12
  356.4 8.5 %copy-start.14 = (s32[8]{0:T(128)}, s32[8]{0:T(128)S(1)}, u32[]{:S(2)}) copy-start(s32[8]{0:T(128)S(1)} %get-tuple-element.1072) | copy-start | bytes 100
  356.4 13.6 %copy-start.9 = (f32[8,3,128]{2,1,0:T(4,128)}, f32[8,3,128]{2,1,0:T(4,128)S(1)}, u32[]{:S(2)}) copy-start(f32[8,3,128]{2,1,0:T(4,128)S(1)} %get-tuple-element.412) | copy-start | bytes 36868
  356.4 7.1 %collective-permute-start.17 = (f32[1,128,128]{2,1,0:T(8,128)S(1)}, f32[1,128,128]{2,1,0:T(8,128)S(1)}, u32[]{:S(2)}, u32[]{:S(2)}) collective-permute-start(f32[1,128,128]{2,1,0:T(8,128)S(1)} %convolution_bitcast_fusion.1), channel_id=1, source_target_pairs={{0,1},{1,2},{2,3},{3,4},{4,5},{5,6},{6,7},{7,8},{8,9},{9,10},{10,1... | collective-permute-start | bytes 196616 | tf_op jit(solution)/shard_map/ppermute | solution.py:22
  359.2 4.4 collective-permute-start.18
  359.2 5.7 collective-permute-start.19
  440.9 14.0 %copy-start.25 = (s32[128]{0:T(128)S(1)}, s32[128]{0:T(128)}, u32[]{:S(2)}) copy-start(s32[128]{0:T(128)} %add_select_fusion.3) | copy-start | bytes 1540
  441.0 14.0 %copy-start.28 = (pred[128]{0:T(512)(128)(4,1)S(1)}, pred[128]{0:T(512)(128)(4,1)}, u32[]{:S(2)}) copy-start(pred[128]{0:T(512)(128)(4,1)} %iota_compare_fusion.7) | copy-start | bytes 388
  441.0 37.1 %copy-start.18 = (f32[128]{0:T(128)S(1)}, f32[128]{0:T(128)}, u32[]{:S(2)}) copy-start(f32[128]{0:T(128)} %get-tuple-element.711) | copy-start | bytes 1540
  441.0 37.1 %copy-start.20 = (f32[128]{0:T(128)S(1)}, f32[128]{0:T(128)}, u32[]{:S(2)}) copy-start(f32[128]{0:T(128)} %get-tuple-element.712) | copy-start | bytes 1540
  441.0 37.0 %copy-start.22 = (f32[128]{0:T(128)S(1)}, f32[128]{0:T(128)}, u32[]{:S(2)}) copy-start(f32[128]{0:T(128)} %broadcast_add_fusion) | copy-start | bytes 1540
  443.2 62.3 %copy-start.15 = (s32[8]{0:T(128)S(1)}, s32[8]{0:T(128)}, u32[]{:S(2)}) copy-start(s32[8]{0:T(128)} %copy-done.14) | copy-start | bytes 100
  443.3 5.3 collective-permute-start.22
  443.7 4.8 collective-permute-start.23
  445.1 4.7 collective-permute-start.24
  448.5 6.4 %collective-permute-start.25 = (f32[1,128,128]{2,1,0:T(8,128)S(1)}, f32[1,128,128]{2,1,0:T(8,128)S(1)}, u32[]{:S(2)}, u32[]{:S(2)}) collective-permute-start(f32[1,128,128]{2,1,0:T(8,128)S(1)} %get-tuple-element.671), channel_id=1, source_target_pairs={{0,2},{1,3},{2,4},{3,5},{4,6},{5,7},{6,8},{7,9},{8,10},{9,11},{10,... | collective-permute-start | bytes 196616 | tf_op jit(solution)/shard_map/ppermute | solution.py:22
  485.2 18.6 %all-to-all-start.11 = ((f32[64,2,1,1,128]{4,1,3,2,0:T(2,128)}), f32[64,2,1,1,128]{4,1,3,2,0:T(2,128)S(1)}, u32[]{:S(2)}, u32[]{:S(2)}) async-start(f32[64,2,1,1,128]{4,1,3,2,0:T(2,128)} %copy.83), calls=%async_computation.11 | async-start | bytes 131072 | tf_op jit(solution)/shard_map/all_to_all | solution.py:53
  491.7 1.7 collective-permute-start.30
  492.5 3.4 collective-permute-start.31
  505.0 51.6 %collective-permute-start.26 = (f32[1,128,128]{2,1,0:T(8,128)S(1)}, f32[1,128,128]{2,1,0:T(8,128)S(1)}, u32[]{:S(2)}, u32[]{:S(2)}) collective-permute-start(f32[1,128,128]{2,1,0:T(8,128)S(1)} %convolution_bitcast_fusion), channel_id=1, source_target_pairs={{0,2},{1,3},{2,4},{3,5},{4,6},{5,7},{6,8},{7,9},{8,10},{9,11},{10,... | collective-permute-start | bytes 196616 | tf_op jit(solution)/shard_map/ppermute | solution.py:22
  549.3 7.3 %collective-permute-start.27 = (f32[1,128,128]{2,1,0:T(8,128)S(1)}, f32[1,128,128]{2,1,0:T(8,128)S(1)}, u32[]{:S(2)}, u32[]{:S(2)}) collective-permute-start(f32[1,128,128]{2,1,0:T(8,128)S(1)} %convolution_bitcast_fusion), channel_id=1, source_target_pairs={{0,1},{1,2},{2,3},{3,4},{4,5},{5,6},{6,7},{7,8},{8,9},{9,10},{10,1... | collective-permute-start | bytes 196616 | tf_op jit(solution)/shard_map/ppermute | solution.py:22
  552.0 4.6 collective-permute-start.28
  552.0 6.0 collective-permute-start.29
  (15 other events, 28.7 us)
